TPU v7x, 32 devices: a whole 2x2x4 slice. The times are simulated.
32 devices in a mesh: batch: 8 (over z, y), tok: 4 (over x, core).
Axes of the slice: x: 2, y: 2, z: 4, core: 2. Of those that a mesh axis runs over, the one named last changes fastest.
Arguments:
- tables: bfloat16 [48, 512, 128], P('tok'), may hold values from -3 to 3
- feature_ids: int32 [128, 48, 8], P('batch', 'tok'), may hold values from 0 to 511
- bag_lengths: int32 [128, 48], P('batch', 'tok'), may hold values from 1 to 8
- table_token: int32 [48], replicated, may hold values from 0 to 15, as said below
- projection: bfloat16 [16, 128, 1536], P('tok'), may hold values from -0.5 to 0.5
- mix_gain: float32 [16, 1536], P('tok'), may hold values from 0.5 to 1.5
- in_weight: bfloat16 [16, 1536, 6144], P('tok', None, 'batch'), may hold values from -0.15625 to 0.15625
- in_bias: float32 [16, 6144], P('tok', 'batch'), may hold values from -3 to 3
- out_weight: bfloat16 [16, 6144, 1536], P('tok', 'batch'), may hold values from -0.078125 to 0.078125
- out_bias: float32 [16, 1536], P('tok'), may hold values from -3 to 3
- out_gain: float32 [16, 1536], P('tok'), may hold values from 0.5 to 1.5
- upstream: bfloat16 [128, 16, 1536], P('batch', 'tok'), may hold values from -6 to 6
Outputs:
- result: bfloat16 [128, 16, 1536], P('batch', 'tok')
- grad_in: bfloat16 [16, 1536, 6144], P('tok', None, 'batch')
- grad_out: bfloat16 [16, 6144, 1536], P('tok', 'batch')
- grad_projection: float32 [16, 128, 1536], P('tok')
Inputs may be any that keep to these rules, and one draw needn't show every extreme that they name: `table_token`: every token 0 to 15 is fed by at least one table.
All inputs are finite; a program needn't handle non-finite values.
Results may differ from a plain program's by a relative error of at most 0.02.
Values may be sent and summed in bfloat16 or wider, within the bound.
A program may use at most 128 MiB of HBM per device.

v0:
```python
import jax
import jax.numpy as jnp
from jax import lax
from jax.sharding import PartitionSpec as P

epsilon = 1e-05


def activate(values):
    return jax.nn.gelu(values, approximate=True)


def activate_slope(values):
    _, pullback = jax.vjp(activate, values)
    return pullback(jnp.ones_like(values))[0]


def normalize(values, gain):
    center = values - jnp.mean(values, axis=-1, keepdims=True)
    scale_inv = lax.rsqrt(jnp.mean(center * center, axis=-1, keepdims=True) + epsilon)
    return center * scale_inv * gain


def normalize_back(values, gain, upper):
    center = values - jnp.mean(values, axis=-1, keepdims=True)
    scale_inv = lax.rsqrt(jnp.mean(center * center, axis=-1, keepdims=True) + epsilon)
    unit = center * scale_inv
    scaled = upper * gain
    return scale_inv * (
        scaled
        - jnp.mean(scaled, axis=-1, keepdims=True)
        - unit * jnp.mean(scaled * unit, axis=-1, keepdims=True)
    )


def pool_table(table_rows, row_index, bag_length):
    picked = jnp.take(table_rows, row_index, axis=0).astype(jnp.float32)
    keeper = (
        jnp.arange(row_index.shape[-1], dtype=jnp.int32)[None, :] < bag_length[:, None]
    ).astype(jnp.float32)
    return jnp.sum(picked * keeper[:, :, None], axis=1)


def local(
    tables,
    feature_ids,
    bag_lengths,
    table_token,
    projection,
    mix_gain,
    in_weight,
    in_bias,
    out_weight,
    out_bias,
    out_gain,
    upstream,
):
    token_rank = lax.axis_index("tok")
    local_tokens, embed_width, model_width = projection.shape
    all_tokens = local_tokens * lax.axis_size("tok")
    head_dim = model_width // all_tokens
    local_tables = tables.shape[0]
    local_rows = feature_ids.shape[0]
    pooled = jax.vmap(pool_table, in_axes=(0, 1, 1))(tables, feature_ids, bag_lengths)
    local_owner = lax.dynamic_slice_in_dim(table_token, token_rank * local_tables, local_tables)
    selector = (local_owner[:, None] == jnp.arange(all_tokens, dtype=jnp.int32)[None, :]).astype(
        jnp.float32
    )
    partial_groups = jnp.einsum("fbc,ft->btc", pooled, selector, precision=lax.Precision.HIGHEST)
    head_weights = projection.reshape(local_tokens, embed_width, all_tokens, head_dim)
    column_weights = lax.all_to_all(head_weights, "tok", split_axis=2, concat_axis=0, tiled=True)
    group_all = lax.psum(partial_groups, "tok").astype(jnp.bfloat16)
    grouped = lax.dynamic_slice_in_dim(group_all, token_rank * local_tokens, local_tokens, 1)
    own_tokens = jnp.einsum(
        "btc,tcd->btd", grouped, projection, preferred_element_type=jnp.float32
    ).astype(jnp.bfloat16)
    mixed_tokens = jnp.einsum(
        "btc,tchk->bhtk", group_all, column_weights, preferred_element_type=jnp.float32
    ).astype(jnp.bfloat16)
    mixed_tokens = mixed_tokens.reshape(local_rows, local_tokens, model_width)
    summed = mixed_tokens.astype(jnp.float32) + own_tokens.astype(jnp.float32)
    normed = normalize(summed, mix_gain[None]).astype(jnp.bfloat16)
    normed_all = lax.all_gather(normed, "batch", axis=0, tiled=True)
    hidden_pre = (
        jnp.einsum("btd,tdf->btf", normed_all, in_weight, preferred_element_type=jnp.float32)
        + in_bias[None]
    )
    hidden = activate(hidden_pre).astype(jnp.bfloat16)
    picked = hidden
    down_own = lax.psum_scatter(
        jnp.einsum("btf,tfd->btd", picked, out_weight, preferred_element_type=jnp.float32),
        "batch",
        scatter_dimension=0,
        tiled=True,
    )
    output_own = down_own + out_bias[None] + normed.astype(jnp.float32)
    result = normalize(output_own, out_gain[None]).astype(jnp.bfloat16)
    upper_grad = normalize_back(output_own, out_gain[None], upstream.astype(jnp.float32)).astype(
        jnp.bfloat16
    )
    upper_all = lax.all_gather(upper_grad, "batch", axis=0, tiled=True)
    grad_out = jnp.einsum(
        "btf,btd->tfd", hidden, upper_all, preferred_element_type=jnp.float32
    ).astype(jnp.bfloat16)
    hidden_grad = (
        jnp.einsum("btd,tfd->btf", upper_all, out_weight, preferred_element_type=jnp.float32)
        * activate_slope(hidden_pre)
    ).astype(jnp.bfloat16)
    grad_in = jnp.einsum(
        "btd,btf->tdf", normed_all, hidden_grad, preferred_element_type=jnp.float32
    ).astype(jnp.bfloat16)
    picked = hidden_grad
    normed_grad = lax.psum_scatter(
        jnp.einsum("btf,tdf->btd", picked, in_weight, preferred_element_type=jnp.float32).astype(
            jnp.bfloat16
        ),
        "batch",
        scatter_dimension=0,
        tiled=True,
    ).astype(jnp.float32) + upper_grad.astype(jnp.float32)
    sum_grad = normalize_back(summed, mix_gain[None], normed_grad).astype(jnp.bfloat16)
    sum_blocks = sum_grad.reshape(local_rows, local_tokens, all_tokens, head_dim)
    head_back = lax.all_to_all(sum_blocks, "tok", split_axis=2, concat_axis=1, tiled=True)
    own_back = jnp.transpose(sum_blocks, (0, 2, 1, 3))
    token_grad = (head_back.astype(jnp.float32) + own_back.astype(jnp.float32)).astype(jnp.bfloat16)
    grad_part = jnp.einsum(
        "btc,bhtk->tchk", grouped, token_grad, preferred_element_type=jnp.float32
    )
    grad_part = grad_part.reshape(local_tokens, embed_width, model_width)
    grad_projection = lax.psum(grad_part.astype(jnp.bfloat16), "batch").astype(jnp.float32)
    return (result, grad_in, grad_out, grad_projection)


def solution(mesh):
    in_specs = (
        P("tok", None, None),
        P("batch", "tok", None),
        P("batch", "tok"),
        P(),
        P("tok", None, None),
        P("tok", None),
        P("tok", None, "batch"),
        P("tok", "batch"),
        P("tok", "batch", None),
        P("tok", None),
        P("tok", None),
        P("batch", "tok", None),
    )
    out_specs = (
        P("batch", "tok", None),
        P("tok", None, "batch"),
        P("tok", "batch", None),
        P("tok", None, None),
    )
    return jax.shard_map(local, mesh=mesh, in_specs=in_specs, out_specs=out_specs, check_vma=False)
```

profile of v0, /device:TPU:0, one launch (start us, length us, event | category | flops | bytes accessed | tf_op | source)
XLA Modules:
  0.0 418.1 jit_solution(7147929013493467835)
XLA Ops:
  7.2 0.0 copy-start
  7.2 2.0 copy.46
  9.2 1.3 copy.47
  10.5 4.5 %all-to-all-start = ((bf16[4,128,16,96]{1,3,0,2:T(8,128)(2,1)}), bf16[4,128,16,96]{1,3,0,2:T(8,128)(2,1)}, u32[]{:S(2)}, u32[]{:S(2)}) async-start(bf16[4,128,16,96]{1,3,0,2:T(8,128)(2,1)} %copy.47), calls=%async_computation | async-start | bytes 3145728 | tf_op jit(solution)/shard_map/all_to_all | solution.py:71
  15.0 0.0 all-gather.3.cloned.1.call-start
  15.1 0.1 copy.44
  15.2 0.1 copy.43
  15.3 0.1 reshape.84
  15.4 0.1 copy.42
  15.6 0.0 copy-start.15
  15.6 8.5 %gather_fusion = bf16[1536,128]{1,0:T(8,128)(2,1)S(1)} fusion(bf16[12,512,128]{2,1,0:T(8,128)(2,1)S(1)} %copy-done, s32[1536]{0:T(1024)S(1)} %reshape.84), kind=kCustom, calls=%fused_computation | custom fusion | bytes 798720 | tf_op jit(solution)/shard_map/vmap(jit(_take))/gather | solution.py:37
  24.1 0.1 dynamic_slice.6
  24.1 0.1 fusion.22
  24.2 0.6 multiply_reduce_fusion
  24.8 0.2 convolution_bitcast_fusion.1
  25.1 17.1 %all-reduce.4 = bf16[16,16,128]{2,1,0:T(8,128)(2,1)S(1)} all-reduce(f32[16,16,128]{2,1,0:T(8,128)S(1)} %convolution_bitcast_fusion.1), channel_id=1, replica_groups=mesh['batch'=8,'tok'=4] {'tok'}, use_global_device_ids=true, to_apply=%region_1.2 | all-reduce | flops 32768 | bytes 196608 | tf_op jit(solution)/shard_map/psum | solution.py:72
  42.2 1.6 copy.49
  43.8 0.0 copy-start.2
  43.8 1.1 fusion.15
  44.9 0.3 copy.51
  45.2 0.2 reshape.81
  45.4 0.0 copy-start.9
  45.5 0.0 copy-start.10
  45.5 0.4 fusion.32
  45.9 0.2 multiply_reduce_fusion.4
  46.1 0.1 copy-done.9
  46.2 0.8 multiply_convert_fusion.3
  47.0 0.0 all-gather.3.cloned.1.call-update
  47.0 0.0 reduce-scatter.3.cloned.1.call-start
  47.1 47.1 %all-gather.3.cloned.1.call-done = bf16[128,4,1536]{2,0,1:T(8,128)(2,1)} async-done(((bf16[16,4,1536]{2,0,1:T(8,128)(2,1)}), bf16[128,4,1536]{2,0,1:T(8,128)(2,1)}) %all-gather.3.cloned.1.call-update) | async-done | bytes 1572880 | tf_op jit(solution)/shard_map/all_gather | solution.py:83
  94.2 5.6 %convolution_add_fusion = f32[4,128,768]{2,1,0:T(8,128)S(1)} fusion(bf16[128,4,1536]{2,0,1:T(8,128)(2,1)} %all-gather.3.cloned.1.call-done, bf16[4,1536,768]{2,1,0:T(8,128)(2,1)} %param.18, f32[4,768]{1,0:T(4,128)S(1)} %copy-done.10), kind=kOutput, calls=%fused_computation.25 | convolution fusion | flops 1208352768 | bytes 12595200 | tf_op jit(solution)/shard_map/btd,tdf->btf/dot_general | solution.py:85
  99.8 7.0 %convolution_bitcast_fusion = f32[128,4,1536]{2,0,1:T(8,128)} fusion(bf16[4,768,1536]{2,1,0:T(8,128)(2,1)} %param.20, f32[4,128,768]{2,1,0:T(8,128)S(1)} %convolution_add_fusion), kind=kOutput, calls=%fused_computation.3 | convolution fusion | flops 1211498496 | bytes 14155776 | tf_op jit(solution)/shard_map/btf,tfd->btd/dot_general | solution.py:91
  106.8 0.0 reduce-scatter.3.cloned.1.call-update
  106.8 0.0 copy-start.7
  106.8 0.0 copy-start.12
  106.8 0.0 all-gather.5.cloned.1.call-start
  106.9 72.8 %reduce-scatter.3.cloned.1.call-done = f32[16,4,1536]{2,0,1:T(8,128)} async-done(((f32[128,4,1536]{2,0,1:T(8,128)}), f32[16,4,1536]{2,0,1:T(8,128)}) %reduce-scatter.3.cloned.1.call-update) | async-done | bytes 393232 | tf_op jit(solution)/shard_map/reduce_scatter | solution.py:90
  179.7 1.2 fusion.31
  180.9 0.2 multiply_reduce_fusion.3
  181.1 0.2 fusion.17
  181.3 1.0 multiply_convert_fusion.1
  182.3 0.0 all-gather.5.cloned.1.call-update
  182.3 0.0 reduce-scatter.5.cloned.1.call-start
  182.3 43.4 %all-gather.5.cloned.1.call-done = bf16[128,4,1536]{2,0,1:T(8,128)(2,1)} async-done(((bf16[16,4,1536]{2,0,1:T(8,128)(2,1)}), bf16[128,4,1536]{2,0,1:T(8,128)(2,1)}) %all-gather.5.cloned.1.call-update) | async-done | bytes 1572880 | tf_op jit(solution)/shard_map/all_gather | solution.py:101
  225.7 7.4 %fusion.11 = bf16[128,4,768]{2,0,1:T(8,128)(2,1)S(1)} fusion(f32[4,128,768]{2,1,0:T(8,128)S(1)} %convolution_add_fusion, bf16[128,4,1536]{2,0,1:T(8,128)(2,1)} %all-gather.5.cloned.1.call-done, bf16[4,768,1536]{2,1,0:T(8,128)(2,1)} %param.20), kind=kOutput, calls=%fused_computation.20 | convolution fusion | flops 1215430656 | bytes 13369344 | tf_op jit(solution)/shard_map/btd,tfd->btf/dot_general | solution.py:106
  233.2 8.2 %fusion = bf16[128,4,1536]{2,0,1:T(8,128)(2,1)} fusion(bf16[128,4,768]{2,0,1:T(8,128)(2,1)S(1)} %fusion.11, bf16[4,1536,768]{2,1,0:T(8,128)(2,1)} %param.18), kind=kOutput, calls=%fused_computation.5 | convolution fusion | flops 1208745984 | bytes 11796480 | tf_op jit(solution)/shard_map/btf,tdf->btd/dot_general | solution.py:114
  241.4 0.0 reduce-scatter.5.cloned.1.call-update
  241.4 64.1 %reduce-scatter.5.cloned.1.call-done = bf16[16,4,1536]{2,0,1:T(8,128)(2,1)} async-done(((bf16[128,4,1536]{2,0,1:T(8,128)(2,1)}), bf16[16,4,1536]{2,0,1:T(8,128)(2,1)}) %reduce-scatter.5.cloned.1.call-update) | async-done | bytes 196624 | tf_op jit(solution)/shard_map/reduce_scatter | solution.py:113
  305.5 1.1 fusion.18
  306.7 1.1 multiply_convert_fusion
  307.8 0.2 reshape.80
  308.0 0.8 copy.55
  308.8 3.6 all-to-all-start.1
  312.4 0.0 all-reduce.3.cloned.1.call-start
  312.5 5.9 %all-to-all-done.1 = bf16[16,4,16,96]{3,0,1,2:T(8,128)(2,1)S(1)} async-done(((bf16[16,4,16,96]{3,0,1,2:T(8,128)(2,1)}), bf16[16,4,16,96]{3,0,1,2:T(8,128)(2,1)S(1)}, u32[]{:S(2)}, u32[]{:S(2)}) %all-to-all-start.1) | async-done | bytes 196640 | tf_op jit(solution)/shard_map/all_to_all | solution.py:123
  318.4 0.7 convolution_convert_fusion.4
  319.2 1.6 copy.59
  320.8 0.0 all-reduce.3.cloned.1.call-update
  320.8 0.8 copy.60
  321.6 0.6 copy-done.3
  322.2 6.4 %convolution_convert_fusion.1 = bf16[4,1536,768]{2,1,0:T(8,128)(2,1)} fusion(bf16[128,4,1536]{2,0,1:T(8,128)(2,1)S(1)} %copy-done.3, bf16[128,4,768]{2,0,1:T(8,128)(2,1)} %copy-done.4), kind=kOutput, calls=%fused_computation.2 | convolution fusion | flops 1212678144 | bytes 11796480 | tf_op jit(solution)/shard_map/btd,btf->tdf/dot_general | solution.py:109
  328.7 5.2 %convolution_convert_fusion = bf16[4,768,1536]{2,1,0:T(8,128)(2,1)} fusion(bf16[128,4,1536]{2,0,1:T(8,128)(2,1)S(1)} %copy-done.6, f32[4,128,768]{2,1,0:T(8,128)S(1)} %convolution_add_fusion), kind=kOutput, calls=%fused_computation.1 | convolution fusion | flops 1216217088 | bytes 12582912 | tf_op jit(solution)/shard_map/btf,btd->tfd/dot_general | solution.py:102
  333.8 74.2 %all-reduce.3.cloned.1.call-done = bf16[4,128,1536]{2,1,0:T(8,128)(2,1)} async-done(((bf16[4,128,1536]{2,1,0:T(8,128)(2,1)}), bf16[4,128,1536]{2,1,0:T(8,128)(2,1)}) %all-reduce.3.cloned.1.call-update) | async-done | bytes 1572880 | tf_op jit(solution)/shard_map/psum | solution.py:130
  408.1 3.5 convert_element_type.142
  (37 shorter events, 0.3 us)
Async XLA Ops:
  7.2 8.4 %copy-start = (bf16[12,512,128]{2,1,0:T(8,128)(2,1)S(1)}, bf16[12,512,128]{2,1,0:T(8,128)(2,1)}, u32[]{:S(2)}) copy-start(bf16[12,512,128]{2,1,0:T(8,128)(2,1)} %param.12) | copy-start | bytes 4718596
  10.5 4.5 %copy-start.11 = (s32[16,12,8]{0,2,1:T(8,128)S(1)}, s32[16,12,8]{0,2,1:T(8,128)}, u32[]{:S(2)}) copy-start(s32[16,12,8]{0,2,1:T(8,128)} %param.13) | copy-start | bytes 18436
  10.5 4.6 %copy-start.14 = (s32[16,12]{1,0:T(8,128)S(1)}, s32[16,12]{1,0:T(8,128)}, u32[]{:S(2)}) copy-start(s32[16,12]{1,0:T(8,128)} %param.14) | copy-start | bytes 2308
  10.5 31.7 %all-to-all-start = ((bf16[4,128,16,96]{1,3,0,2:T(8,128)(2,1)}), bf16[4,128,16,96]{1,3,0,2:T(8,128)(2,1)}, u32[]{:S(2)}, u32[]{:S(2)}) async-start(bf16[4,128,16,96]{1,3,0,2:T(8,128)(2,1)} %copy.47), calls=%async_computation | async-start | bytes 3145728 | tf_op jit(solution)/shard_map/all_to_all | solution.py:71
  15.0 79.2 %all-gather.3.cloned.1.call-start = ((), (), s32[]{:S(2)}) async-start(), calls=%async_computation.4 | async-start | bytes 1769472 | tf_op jit(solution)/shard_map/all_gather | solution.py:83
  15.6 8.5 %copy-start.15 = (s32[48]{0:T(128)S(1)}, s32[48]{0:T(128)}, u32[]{:S(2)}) copy-start(s32[48]{0:T(128)} %param.15) | copy-start | bytes 580
  43.8 1.6 copy-start.2
  45.4 0.7 copy-start.9
  45.5 48.7 %copy-start.10 = (f32[4,768]{1,0:T(4,128)S(1)}, f32[4,768]{1,0:T(4,128)}, u32[]{:S(2)}) copy-start(f32[4,768]{1,0:T(4,128)} %param.19) | copy-start | bytes 36868
  47.0 132.7 %reduce-scatter.3.cloned.1.call-start = ((), (), s32[]{:S(2)}) async-start(), calls=%async_computation.5 | async-start | bytes 3538944 | tf_op jit(solution)/shard_map/reduce_scatter | solution.py:90
  106.8 72.9 %copy-start.13 = (f32[4,1536]{1,0:T(4,128)S(1)}, f32[4,1536]{1,0:T(4,128)}, u32[]{:S(2)}) copy-start(f32[4,1536]{1,0:T(4,128)} %param.21) | copy-start | bytes 73732
  106.8 74.3 %copy-start.7 = (bf16[16,4,1536]{2,1,0:T(4,128)(2,1)S(1)}, bf16[16,4,1536]{2,1,0:T(4,128)(2,1)}, u32[]{:S(2)}) copy-start(bf16[16,4,1536]{2,1,0:T(4,128)(2,1)} %param.23) | copy-start | bytes 589828
  106.8 74.3 %copy-start.12 = (f32[4,1536]{1,0:T(4,128)S(1)}, f32[4,1536]{1,0:T(4,128)}, u32[]{:S(2)}) copy-start(f32[4,1536]{1,0:T(4,128)} %param.22) | copy-start | bytes 73732
  106.8 118.9 %all-gather.5.cloned.1.call-start = ((), (), s32[]{:S(2)}) async-start(), calls=%async_computation.6 | async-start | bytes 1769472 | tf_op jit(solution)/shard_map/all_gather | solution.py:101
  182.3 123.2 %reduce-scatter.5.cloned.1.call-start = ((), (), s32[]{:S(2)}) async-start(), calls=%async_computation.7 | async-start | bytes 1769472 | tf_op jit(solution)/shard_map/reduce_scatter | solution.py:113
  233.2 8.2 %copy-start.4 = (bf16[128,4,768]{2,0,1:T(8,128)(2,1)}, bf16[128,4,768]{2,0,1:T(8,128)(2,1)S(1)}, u32[]{:S(2)}) copy-start(bf16[128,4,768]{2,0,1:T(8,128)(2,1)S(1)} %fusion.11) | copy-start | bytes 2359300
  241.4 64.1 %copy-start.5 = (bf16[16,4,1536]{2,0,1:T(8,128)(2,1)S(1)}, bf16[16,4,1536]{2,0,1:T(8,128)(2,1)}, u32[]{:S(2)}) copy-start(bf16[16,4,1536]{2,0,1:T(8,128)(2,1)} %get-tuple-element.22) | copy-start | bytes 589828
  308.8 9.6 %all-to-all-start.1 = ((bf16[16,4,16,96]{3,0,1,2:T(8,128)(2,1)}), bf16[16,4,16,96]{3,0,1,2:T(8,128)(2,1)S(1)}, u32[]{:S(2)}, u32[]{:S(2)}) async-start(bf16[16,4,16,96]{3,0,1,2:T(8,128)(2,1)} %copy.55), calls=%async_computation.3 | async-start | bytes 524288 | tf_op jit(solution)/shard_map/all_to_all | solution.py:123
  312.4 95.7 %all-reduce.3.cloned.1.call-start = ((), (), s32[]{:S(2)}) async-start(), calls=%async_computation.8 | async-start | bytes 3145728 | tf_op jit(solution)/shard_map/psum | solution.py:130
  319.2 1.6 copy-start.8
  320.8 1.5 copy-start.3
  322.2 6.4 %copy-start.6 = (bf16[128,4,1536]{2,0,1:T(8,128)(2,1)S(1)}, bf16[128,4,1536]{2,0,1:T(8,128)(2,1)}, u32[]{:S(2)}) copy-start(bf16[128,4,1536]{2,0,1:T(8,128)(2,1)} %all-gather.5.cloned.1.call-done) | copy-start | bytes 4718596
  328.7 82.9 %copy-start.1 = (bf16[12,512,128]{2,1,0:T(8,128)(2,1)S(1)}, bf16[12,512,128]{2,1,0:T(8,128)(2,1)}, u32[]{:S(2)}) copy-start(bf16[12,512,128]{2,1,0:T(8,128)(2,1)} %param.12) | copy-start | bytes 4718596
Sparse Core Ops, SparseCore 0:
  47.1 47.0 all-gather.2
  106.9 72.7 reduce-scatter.2
  182.4 43.2 all-gather.4
  241.6 63.9 reduce-scatter.4
  320.9 87.1 all-reduce.2
where the time goes:
time: 419 us; the launch traced here: 418 us
  waiting for transfers between devices  308 us (74%)
  matrix products  42.2 us (10%)
  local copies, waits for them, and re-layouts  18.7 us (4%)
  blocking collectives  17.1 us (4%)
  between operations  14.1 us (3%)
  other arithmetic  10.1 us (2%)
  starting transfers between devices  8.28 us (2%)
    psum x1, waiting for transfers between devices, local(): lax.psum(grad_part.astype(jnp.bfloat16), 'batch').astype(jnp.float32)  74.2 us
    reduce_scatter x1, waiting for transfers between devices, local(): lax.psum_scatter(jnp.einsum('btf,tfd->btd', picked, out_weight, preferred...  72.8 us
    reduce_scatter x1, waiting for transfers between devices, local(): lax.psum_scatter(jnp.einsum('btf,tdf->btd', picked, in_weight, preferred_...  64.1 us
    all_gather x1, waiting for transfers between devices, local(): normed_all = lax.all_gather(normed, 'batch', axis=0, tiled=True)  47.1 us
    all_gather x1, waiting for transfers between devices, local(): upper_all = lax.all_gather(upper_grad, 'batch', axis=0, tiled=True)  43.4 us
    psum x1, blocking collectives, local(): group_all = lax.psum(partial_groups, 'tok').astype(jnp.bfloat16)  17.1 us
    gather x3, local copies, waits for them, and re-layouts, pool_table(): picked = jnp.take(table_rows, row_index, axis=0).astype(jnp.float32)  8.66 us
  transfers between devices with their start and end apart: 7, of which 6 were waited for; matrix products, arithmetic and copies ran while one was open for 5% of the time, Pallas kernels for 0%

commit v1 on v0

v1 whole, which is shorter than its diff:
```python
import functools
import math

import jax
import jax.numpy as jnp
from jax import lax
from jax.experimental import pallas as pl
from jax.experimental.pallas import tpu as pltpu
from jax.sharding import PartitionSpec as P

epsilon = 1e-05


def normalize(values, gain):
    center = values - jnp.mean(values, axis=-1, keepdims=True)
    scale_inv = lax.rsqrt(jnp.mean(center * center, axis=-1, keepdims=True) + epsilon)
    return center * scale_inv * gain


def normalize_back(values, gain, upper):
    center = values - jnp.mean(values, axis=-1, keepdims=True)
    scale_inv = lax.rsqrt(jnp.mean(center * center, axis=-1, keepdims=True) + epsilon)
    unit = center * scale_inv
    scaled = upper * gain
    return scale_inv * (
        scaled
        - jnp.mean(scaled, axis=-1, keepdims=True)
        - unit * jnp.mean(scaled * unit, axis=-1, keepdims=True)
    )


def pool_table(table_rows, row_index, bag_length):
    picked = jnp.take(table_rows, row_index, axis=0).astype(jnp.float32)
    keeper = (
        jnp.arange(row_index.shape[-1], dtype=jnp.int32)[None, :] < bag_length[:, None]
    ).astype(jnp.float32)
    return jnp.sum(picked * keeper[:, :, None], axis=1)


def remote(source, target, send, recv, peer):
    return pltpu.make_async_remote_copy(
        src_ref=source,
        dst_ref=target,
        send_sem=send,
        recv_sem=recv,
        device_id={"batch": peer},
        device_id_type=pl.DeviceIdType.MESH,
    )


class Ring:
    def __init__(self, count):
        self.far_count = count // 2
        rank = lax.axis_index("batch")
        self.far = rank // 2
        self.near = rank % 2
        self.partner = self.far * 2 + (1 - self.near)

    def after(self, step):
        return (self.far + step) % self.far_count

    def peer(self, step):
        return self.after(step) * 2 + self.near

    def greet(self):
        barrier = pltpu.get_barrier_semaphore()
        for device in [self.partner] + [self.peer(k) for k in range(1, self.far_count)]:
            pl.semaphore_signal(
                barrier, inc=1, device_id={"batch": device}, device_id_type=pl.DeviceIdType.MESH
            )
        pl.semaphore_wait(barrier, self.far_count)


class Gather:
    def __init__(self, ring, own, full, local_sem, far_send, far_recv, near_send, near_recv):
        self.ring, self.own, self.full = ring, own, full
        self.local_sem = local_sem
        self.far_send, self.far_recv = far_send, far_recv
        self.near_send, self.near_recv = near_send, near_recv

    def far_copy(self, t, k):
        ring = self.ring
        return remote(
            self.own.at[t],
            self.full.at[t, ring.near, ring.far],
            self.far_send.at[t, k - 1],
            self.far_recv.at[t, k - 1],
            ring.peer(k),
        )

    def own_copy(self, t):
        ring = self.ring
        return pltpu.make_async_copy(
            self.own.at[t], self.full.at[t, ring.near, ring.far], self.local_sem.at[t]
        )

    def near_copy(self, t):
        half = self.full.at[t, self.ring.near]
        return remote(half, half, self.near_send.at[t], self.near_recv.at[t], self.ring.partner)

    def start(self, t):
        for k in range(1, self.ring.far_count):
            self.far_copy(t, k).start()
        self.own_copy(t).start()

    def forward(self, t):
        ring = self.ring
        self.own_copy(t).wait()
        for k in range(1, ring.far_count):
            remote(
                self.own.at[t],
                self.full.at[t, ring.near, ring.after(ring.far_count - k)],
                self.far_send.at[t, k - 1],
                self.far_recv.at[t, k - 1],
                ring.peer(k),
            ).wait_recv()
        self.near_copy(t).start()

    def arrive(self, t):
        half = self.full.at[t, 1 - self.ring.near]
        remote(
            half, half, self.near_send.at[t], self.near_recv.at[t], self.ring.partner
        ).wait_recv()

    def finish(self, t):
        for k in range(1, self.ring.far_count):
            self.far_copy(t, k).wait_send()
        self.near_copy(t).wait_send()


class Scatter:
    def __init__(self, ring, part, first, pair, second, near_send, near_recv, far_send, far_recv):
        self.ring, self.part, self.first = ring, part, first
        self.pair, self.second = pair, second
        self.near_send, self.near_recv = near_send, near_recv
        self.far_send, self.far_recv = far_send, far_recv

    def near_copy(self, t):
        return remote(
            self.part.at[t, 1 - self.ring.near],
            self.first.at[t],
            self.near_send.at[t],
            self.near_recv.at[t],
            self.ring.partner,
        )

    def far_copy(self, t, k):
        return remote(
            self.pair.at[t, self.ring.after(k)],
            self.second.at[t, k - 1],
            self.far_send.at[t, k - 1],
            self.far_recv.at[t, k - 1],
            self.ring.peer(k),
        )

    def start(self, t):
        self.near_copy(t).start()

    def forward(self, t):
        self.near_copy(t).wait_recv()
        mine = self.part[t, self.ring.near].astype(jnp.float32)
        self.pair[t] = (mine + self.first[t].astype(jnp.float32)).astype(self.pair.dtype)
        for k in range(1, self.ring.far_count):
            self.far_copy(t, k).start()

    def total(self, t):
        ring = self.ring
        result = self.part[t, ring.near, ring.far].astype(jnp.float32)
        result = result + self.first[t, ring.far].astype(jnp.float32)
        for k in range(1, ring.far_count):
            self.far_copy(t, k).wait_recv()
            result = result + self.second[t, k - 1].astype(jnp.float32)
        return result

    def finish(self, t):
        self.near_copy(t).wait_send()
        for k in range(1, self.ring.far_count):
            self.far_copy(t, k).wait_send()


def tile_of(width):
    return 256 if width % 256 == 0 else 128


def block_kernel(
    count,
    normed_ref,
    summed_ref,
    mix_gain_ref,
    in_weight_ref,
    in_bias_ref,
    out_weight_ref,
    out_bias_ref,
    out_gain_ref,
    upstream_ref,
    result_ref,
    normed_all_ref,
    hidden_ref,
    upper_all_ref,
    hidden_grad_ref,
    sum_grad_ref,
    in_held,
    out_held,
    slope,
    upper_own,
    part_a,
    first_a,
    pair_a,
    second_a,
    part_b,
    first_b,
    pair_b,
    second_b,
    weight_sem,
    one_sem,
    many_sem,
):
    tokens, rows, width = normed_ref.shape
    units = in_held.shape[-1]
    examples = count * rows
    far_count = count // 2
    ring = Ring(count)
    in_copy = lambda t: pltpu.make_async_copy(in_weight_ref.at[t], in_held.at[t], weight_sem.at[0, t])
    out_copy = lambda t: pltpu.make_async_copy(
        out_weight_ref.at[t], out_held.at[t], weight_sem.at[1, t]
    )
    for t in range(tokens):
        in_copy(t).start()
        out_copy(t).start()
    one = [one_sem.at[i] for i in range(10)]
    many = [many_sem.at[i] for i in range(8)]
    gather_a = Gather(
        ring, normed_ref, normed_all_ref, one[0], many[0], many[1], one[1], one[2]
    )
    gather_b = Gather(
        ring, upper_own, upper_all_ref, one[3], many[2], many[3], one[4], one[5]
    )
    scatter_a = Scatter(
        ring, part_a, first_a, pair_a, second_a, one[6], one[7], many[4], many[5]
    )
    scatter_b = Scatter(
        ring, part_b, first_b, pair_b, second_b, one[8], one[9], many[6], many[7]
    )
    ring.greet()
    for t in range(tokens):
        gather_a.start(t)

    unit_tile = tile_of(units)
    width_tile = tile_of(width)

    def forward(t):
        in_copy(t).wait()
        out_copy(t).wait()
        gather_a.arrive(t)

        @pl.loop(0, units // unit_tile)
        def _(i):
            columns = pl.ds(pl.multiple_of(i * unit_tile, unit_tile), unit_tile)
            value = jnp.dot(
                normed_all_ref[t].reshape(examples, width),
                in_held[t, :, columns],
                preferred_element_type=jnp.float32,
            ) + in_bias_ref[t, :, columns]
            factor = math.sqrt(2 / math.pi)
            square = value * value
            bent = jnp.tanh(factor * (value + 0.044715 * value * square))
            hidden_ref[t, :, columns] = (0.5 * value * (1 + bent)).astype(jnp.bfloat16)
            slope[t, :, columns] = 0.5 * (1 + bent) + 0.5 * value * (1 - bent * bent) * factor * (
                1 + 3 * 0.044715 * square
            )

        @pl.loop(0, width // width_tile)
        def _(i):
            columns = pl.ds(pl.multiple_of(i * width_tile, width_tile), width_tile)
            value = jnp.dot(
                hidden_ref[t], out_held[t, :, columns], preferred_element_type=jnp.float32
            )
            part_a[t, :, :, :, columns] = value.astype(jnp.bfloat16).reshape(
                2, far_count, rows, width_tile
            )

        scatter_a.start(t)

    def turn(t):
        output = scatter_a.total(t) + out_bias_ref[t] + normed_ref[t].astype(jnp.float32)
        center = output - jnp.mean(output, axis=-1, keepdims=True)
        scale_inv = lax.rsqrt(jnp.mean(center * center, axis=-1, keepdims=True) + epsilon)
        result_ref[t] = (center * scale_inv * out_gain_ref[t]).astype(jnp.bfloat16)
        upper_own[t] = normalize_back(
            output, out_gain_ref[t], upstream_ref[t].astype(jnp.float32)
        ).astype(jnp.bfloat16)
        gather_b.start(t)

    def backward(t):
        gather_b.arrive(t)

        @pl.loop(0, units // unit_tile)
        def _(i):
            columns = pl.ds(pl.multiple_of(i * unit_tile, unit_tile), unit_tile)
            value = lax.dot_general(
                upper_all_ref[t].reshape(examples, width),
                out_held[t, columns, :],
                (((1,), (1,)), ((), ())),
                preferred_element_type=jnp.float32,
            )
            hidden_grad_ref[t, :, columns] = (value * slope[t, :, columns]).astype(jnp.bfloat16)

        @pl.loop(0, width // width_tile)
        def _(i):
            columns = pl.ds(pl.multiple_of(i * width_tile, width_tile), width_tile)
            value = lax.dot_general(
                hidden_grad_ref[t],
                in_held[t, columns, :],
                (((1,), (1,)), ((), ())),
                preferred_element_type=jnp.float32,
            )
            part_b[t, :, :, :, columns] = value.astype(jnp.bfloat16).reshape(
                2, far_count, rows, width_tile
            )

        scatter_b.start(t)

    def close(t):
        normed_grad = scatter_b.total(t) + upper_own[t].astype(jnp.float32)
        sum_grad_ref[t] = normalize_back(summed_ref[t], mix_gain_ref[t], normed_grad).astype(
            jnp.bfloat16
        )

    stages = [
        gather_a.forward,
        forward,
        scatter_a.forward,
        turn,
        gather_b.forward,
        backward,
        scatter_b.forward,
        close,
    ]

    def step(s, carry):
        for delay, stage in enumerate(stages):

            @pl.when(jnp.logical_and(s >= delay, s < delay + tokens))
            def _():
                stage(s - delay)

        return carry

    lax.fori_loop(0, tokens + len(stages) - 1, step, 0)
    for t in range(tokens):
        for part in (gather_a, scatter_a, gather_b, scatter_b):
            part.finish(t)


def run_block(count, *operands):
    tokens, rows, width = operands[0].shape
    units = operands[3].shape[-1]
    far_count = count // 2
    half = jnp.bfloat16
    vmem = pl.BlockSpec(memory_space=pltpu.VMEM)
    anywhere = pl.BlockSpec(memory_space=pl.ANY)
    full = (tokens, 2, far_count, rows, width)
    one_way = [
        pltpu.VMEM(full, half),
        pltpu.VMEM((tokens, far_count, rows, width), half),
        pltpu.VMEM((tokens, far_count, rows, width), half),
        pltpu.VMEM((tokens, far_count - 1, rows, width), half),
    ]
    examples = count * rows
    return pl.pallas_call(
        functools.partial(block_kernel, count),
        out_shape=[
            jax.ShapeDtypeStruct((tokens, rows, width), half),
            jax.ShapeDtypeStruct(full, half),
            jax.ShapeDtypeStruct((tokens, examples, units), half),
            jax.ShapeDtypeStruct(full, half),
            jax.ShapeDtypeStruct((tokens, examples, units), half),
            jax.ShapeDtypeStruct((tokens, rows, width), half),
        ],
        in_specs=[vmem, vmem, vmem, anywhere, vmem, anywhere, vmem, vmem, vmem],
        out_specs=[vmem] * 6,
        scratch_shapes=[
            pltpu.VMEM((tokens, width, units), half),
            pltpu.VMEM((tokens, units, width), half),
            pltpu.VMEM((tokens, examples, units), jnp.float32),
            pltpu.VMEM((tokens, rows, width), half),
            *one_way,
            *one_way,
            pltpu.SemaphoreType.DMA((2, tokens)),
            pltpu.SemaphoreType.DMA((10, tokens)),
            pltpu.SemaphoreType.DMA((8, tokens, far_count - 1)),
        ],
        compiler_params=pltpu.CompilerParams(
            collective_id=0, has_side_effects=True, vmem_limit_bytes=50 * 1024 * 1024
        ),
        name="block",
    )(*operands)


def gather_kernel(count, own_ref, full_ref, one_sem, many_sem):
    ring = Ring(count)
    gather = Gather(
        ring, own_ref, full_ref, one_sem.at[0], many_sem.at[0], many_sem.at[1], one_sem.at[1],
        one_sem.at[2],
    )
    ring.greet()
    tokens = own_ref.shape[0]
    for t in range(tokens):
        gather.start(t)
    for t in range(tokens):
        gather.forward(t)
    for t in range(tokens):
        gather.arrive(t)
        gather.finish(t)


def run_gather(count, own):
    tokens, rows, width = own.shape
    far_count = count // 2
    vmem = pl.BlockSpec(memory_space=pltpu.VMEM)
    return pl.pallas_call(
        functools.partial(gather_kernel, count),
        out_shape=jax.ShapeDtypeStruct((tokens, 2, far_count, rows, width), own.dtype),
        in_specs=[vmem],
        out_specs=vmem,
        scratch_shapes=[
            pltpu.SemaphoreType.DMA((3, tokens)),
            pltpu.SemaphoreType.DMA((2, tokens, far_count - 1)),
        ],
        compiler_params=pltpu.CompilerParams(
            collective_id=1, has_side_effects=True, vmem_limit_bytes=16 * 1024 * 1024
        ),
        name="gather",
    )(own)


def local(
    tables,
    feature_ids,
    bag_lengths,
    table_token,
    projection,
    mix_gain,
    in_weight,
    in_bias,
    out_weight,
    out_bias,
    out_gain,
    upstream,
):
    token_rank = lax.axis_index("tok")
    count = lax.axis_size("batch")
    local_tokens, embed_width, model_width = projection.shape
    all_tokens = local_tokens * lax.axis_size("tok")
    head_dim = model_width // all_tokens
    local_tables, table_rows, _ = tables.shape
    local_rows = feature_ids.shape[0]
    keeper = jnp.arange(feature_ids.shape[-1], dtype=jnp.int32) < bag_lengths[:, :, None]
    chosen = jnp.where(keeper, feature_ids, -1)
    uses = jnp.sum(
        (chosen[:, :, :, None] == jnp.arange(table_rows, dtype=jnp.int32)).astype(jnp.float32),
        axis=2,
    ).astype(jnp.bfloat16)
    pooled = jnp.einsum("bfr,frc->fbc", uses, tables, preferred_element_type=jnp.float32)
    local_owner = lax.dynamic_slice_in_dim(table_token, token_rank * local_tables, local_tables)
    selector = (local_owner[:, None] == jnp.arange(all_tokens, dtype=jnp.int32)[None, :]).astype(
        jnp.float32
    )
    partial_groups = jnp.einsum("fbc,ft->tbc", pooled, selector, precision=lax.Precision.HIGHEST)
    group_all = lax.psum(partial_groups, "tok").astype(jnp.bfloat16)
    grouped = lax.dynamic_slice_in_dim(group_all, token_rank * local_tokens, local_tokens, 0)
    own_tokens = jnp.einsum(
        "tbc,tcd->tbd", grouped, projection, preferred_element_type=jnp.float32
    ).astype(jnp.bfloat16)

    def exchange(values):
        blocks = values.reshape(local_tokens, local_rows, all_tokens, head_dim)
        moved = lax.all_to_all(blocks, "tok", split_axis=2, concat_axis=0, tiled=True)
        return jnp.transpose(moved, (2, 1, 0, 3)).reshape(values.shape)

    summed = exchange(own_tokens).astype(jnp.float32) + own_tokens.astype(jnp.float32)
    normed = normalize(summed, mix_gain[:, None]).astype(jnp.bfloat16)
    result, normed_all, hidden, upper_all, hidden_grad, sum_grad = run_block(
        count,
        normed,
        summed,
        mix_gain[:, None],
        in_weight,
        in_bias[:, None],
        out_weight,
        out_bias[:, None],
        out_gain[:, None],
        jnp.transpose(upstream, (1, 0, 2)),
    )
    flat = (local_tokens, count * local_rows, model_width)
    grad_out = jnp.einsum(
        "tbf,tbd->tfd", hidden, upper_all.reshape(flat), preferred_element_type=jnp.float32
    ).astype(jnp.bfloat16)
    grad_in = jnp.einsum(
        "tbd,tbf->tdf", normed_all.reshape(flat), hidden_grad, preferred_element_type=jnp.float32
    ).astype(jnp.bfloat16)
    token_grad = (
        sum_grad.astype(jnp.float32) + exchange(sum_grad).astype(jnp.float32)
    ).astype(jnp.bfloat16)
    both = run_gather(count, jnp.concatenate([token_grad, grouped], axis=-1))
    both = both.reshape(local_tokens, count * local_rows, model_width + embed_width)
    grad_projection = jnp.einsum(
        "tbc,tbd->tcd",
        both[..., model_width:],
        both[..., :model_width],
        preferred_element_type=jnp.float32,
    )
    return (jnp.transpose(result, (1, 0, 2)), grad_in, grad_out, grad_projection)


def solution(mesh):
    in_specs = (
        P("tok", None, None),
        P("batch", "tok", None),
        P("batch", "tok"),
        P(),
        P("tok", None, None),
        P("tok", None),
        P("tok", None, "batch"),
        P("tok", "batch"),
        P("tok", "batch", None),
        P("tok", None),
        P("tok", None),
        P("batch", "tok", None),
    )
    out_specs = (
        P("batch", "tok", None),
        P("tok", None, "batch"),
        P("tok", "batch", None),
        P("tok", None, None),
    )
    return jax.shard_map(local, mesh=mesh, in_specs=in_specs, out_specs=out_specs, check_vma=False)
```

time: 419 us -> 186 us (0.44)
  waiting for transfers between devices: 308 us -> 4.02 us
  Pallas kernels: 0 us -> 125 us
  matrix products: 42.2 us -> 17.7 us
  between operations: 14.1 us -> 0.91 us
  other arithmetic: 10.1 us -> 3.39 us
  local copies, waits for them, and re-layouts: 18.7 us -> 12.2 us
    reduce_scatter x2 -> x0, waiting for transfers between devices: 137 us -> none  [the longest x1 72.8 us: local(): lax.psum_scatter(jnp.einsum('btf,tfd->btd', picked, out_weight, preferred...]
    pallas_call x0 -> x2, Pallas kernels: none -> 125 us  [the longest x1 95.1 us: run_block(): pl.pallas_call(functools.partial(block_kernel, count), out_shape=[jax.Sha...]
    all_gather x2 -> x0, waiting for transfers between devices: 90.5 us -> none  [the longest x1 47.1 us: local(): normed_all = lax.all_gather(normed, 'batch', axis=0, tiled=True)]
    psum x1 -> x0, waiting for transfers between devices: 74.2 us -> none  [local(): lax.psum(grad_part.astype(jnp.bfloat16), 'batch').astype(jnp.float32)]
    dot_general x10 -> x6, matrix products: 42.2 us -> 17.7 us  [the longest x1 7.92 us: local(): jnp.einsum('tbd,tbf->tdf', normed_all.reshape(flat), hidden_grad, preferr...]
    gather x3 -> x0, local copies, waits for them, and re-layouts: 8.66 us -> none  [pool_table(): picked = jnp.take(table_rows, row_index, axis=0).astype(jnp.float32)]
    convert_element_type x6 -> x4, other arithmetic: 6.46 us -> 1.2 us  [the longest x1 0.99 us: local(): exchange(sum_grad).astype(jnp.float32)]
  transfers between devices with their start and end apart: 7 -> 2, of which waited for: 6 -> 1; matrix products, arithmetic and copies ran while one was open for 5% -> 9% of each run, Pallas kernels for 0% -> 0%
where the time goes in v1:
time: 186 us; the launch traced here: 185 us
  Pallas kernels  125 us (67%)
  matrix products  17.7 us (10%)
  blocking collectives  14.5 us (8%)
  local copies, waits for them, and re-layouts  12.2 us (7%)
  starting transfers between devices  7.44 us (4%)
  waiting for transfers between devices  4.02 us (2%)
  other arithmetic  3.39 us (2%)
    pallas_call x1, Pallas kernels, run_block(): pl.pallas_call(functools.partial(block_kernel, count), out_shape=[jax.Sha...  95.1 us
    pallas_call x1, Pallas kernels, run_gather(): pl.pallas_call(functools.partial(gather_kernel, count), out_shape=jax.Sha...  30 us
    psum x1, blocking collectives, local(): group_all = lax.psum(partial_groups, 'tok').astype(jnp.bfloat16)  14.5 us
    dot_general x1, matrix products, local(): jnp.einsum('tbd,tbf->tdf', normed_all.reshape(flat), hidden_grad, preferr...  7.92 us
    all_to_all x2, starting transfers between devices, exchange(): lax.all_to_all(blocks, 'tok', split_axis=2, concat_axis=0, tiled=True)  7.44 us
    unnamed x33, local copies, waits for them, and re-layouts  5.5 us
    dot_general x1, matrix products, local(): jnp.einsum('tbf,tbd->tfd', hidden, upper_all.reshape(flat), preferred_ele...  5.17 us
    all_to_all x2, waiting for transfers between devices, exchange(): lax.all_to_all(blocks, 'tok', split_axis=2, concat_axis=0, tiled=True)  4.02 us
  transfers between devices with their start and end apart: 2, of which 1 were waited for; matrix products, arithmetic and copies ran while one was open for 9% of the time, Pallas kernels for 0%

profile of v1, /device:TPU:0, one launch (start us, length us, event | category | flops | bytes accessed | tf_op | source)
XLA Modules:
  0.0 185.1 jit_solution(6304275066618303026)
XLA Ops:
  0.6 0.0 copy-start
  0.6 0.0 copy-start.14
  0.7 0.9 copy.52
  1.6 0.8 fusion.6
  2.4 0.1 copy.53
  2.5 1.0 convert_reduce_fusion
  3.5 1.8 fusion.2
  5.3 0.0 copy-done.14
  5.3 0.1 dynamic_slice.6
  5.4 0.2 fusion.4
  5.7 14.5 %all-reduce.1 = bf16[16,16,128]{2,1,0:T(8,128)(2,1)S(1)} all-reduce(f32[16,16,128]{2,1,0:T(8,128)S(1)} %copy.56), channel_id=1, replica_groups=mesh['batch'=8,'tok'=4] {'tok'}, use_global_device_ids=true, to_apply=%region_1.2 | all-reduce | flops 32768 | bytes 196608 | tf_op jit(solution)/shard_map/psum | solution.py:470
  20.2 0.0 copy-start.8
  20.2 0.6 copy-done.8
  20.8 0.0 copy-done
  20.8 0.0 copy-start.10
  20.8 0.0 copy-start.13
  20.8 0.0 copy-start.11
  20.8 0.0 copy-start.12
  20.8 0.0 copy-start.7
  20.8 0.3 convolution_convert_fusion.2
  21.1 0.2 reshape.49
  21.4 0.8 copy.57
  22.1 3.4 %all-to-all-start = ((bf16[4,16,16,96]{3,1,0,2:T(8,128)(2,1)}), bf16[4,16,16,96]{3,1,0,2:T(8,128)(2,1)S(1)}, u32[]{:S(2)}, u32[]{:S(2)}) async-start(bf16[4,16,16,96]{3,1,0,2:T(8,128)(2,1)} %copy.57), calls=%async_computation | async-start | bytes 524288 | tf_op jit(solution)/shard_map/all_to_all | solution.py:478
  25.6 0.0 copy-done.10
  25.6 0.6 broadcast_in_dim.13.mix_gain_ref
  26.2 0.0 copy-done.13
  26.2 0.0 copy-done.11
  26.2 0.6 broadcast_in_dim.28.out_bias_ref
  26.9 0.0 copy-done.12
  26.9 0.6 broadcast_in_dim.29.out_gain_ref
  27.5 0.0 copy-done.7
  27.5 4.0 %all-to-all-done = bf16[4,16,16,96]{3,1,0,2:T(8,128)(2,1)S(1)} async-done(((bf16[4,16,16,96]{3,1,0,2:T(8,128)(2,1)}), bf16[4,16,16,96]{3,1,0,2:T(8,128)(2,1)S(1)}, u32[]{:S(2)}, u32[]{:S(2)}) %all-to-all-start) | async-done | bytes 196640 | tf_op jit(solution)/shard_map/all_to_all | solution.py:478
  31.6 0.2 copy.58
  31.8 0.2 reshape.54
  32.0 0.1 fusion.10
  32.2 0.2 multiply_reduce_fusion
  32.4 0.1 multiply_convert_fusion.normed_ref
  32.5 0.0 copy-start.3
  32.5 0.7 copy-done.3
  33.3 0.0 copy-start.4
  33.3 0.7 copy-done.4
  34.0 0.0 copy-start.5
  34.0 0.7 copy-done.5
  34.7 95.1 %block.1 = (bf16[4,16,1536]{2,1,0:T(8,128)(2,1)S(1)}, bf16[4,2,4,16,1536]{4,3,2,1,0:T(8,128)(2,1)}, bf16[4,128,768]{2,1,0:T(8,128)(2,1)S(1)}, bf16[4,2,4,16,1536...) custom-call(bf16[4,16,1536]{2,1,0:T(8,128)(2,1)S(1)} %multiply_convert_fusion.normed_ref, ...), custom_call_target="tpu_custom_call" | custom-call | tf_op jit(solution)/shard_map/block/pallas_call | solution.py:370
  129.8 0.0 copy-start.1
  129.8 0.7 copy-done.1
  130.5 0.9 reshape.52
  131.4 1.7 copy.62
  133.1 4.0 %all-to-all-start.1 = ((bf16[4,16,16,96]{3,1,0,2:T(8,128)(2,1)}), bf16[4,16,16,96]{3,1,0,2:T(8,128)(2,1)}, u32[]{:S(2)}, u32[]{:S(2)}) async-start(bf16[4,16,16,96]{3,1,0,2:T(8,128)(2,1)} %copy.62), calls=%async_computation.1 | async-start | bytes 524288 | tf_op jit(solution)/shard_map/all_to_all | solution.py:478
  137.2 0.0 copy-start.6
  137.2 7.9 %convolution_convert_fusion.1 = bf16[4,1536,768]{2,1,0:T(8,128)(2,1)} fusion(bf16[4,128,1536]{2,1,0:T(8,128)(2,1)} %bitcast.41, bf16[4,128,768]{2,1,0:T(8,128)(2,1)S(1)} %get-tuple-element.12), kind=kOutput, calls=%fused_computation.1 | convolution fusion | flops 1212678144 | bytes 11796480 | tf_op jit(solution)/shard_map/tbd,tbf->tdf/dot_general | solution.py:499
  145.1 0.0 copy-done.6
  145.1 0.0 copy-start.2
  145.1 5.2 %convolution_convert_fusion = bf16[4,768,1536]{2,1,0:T(8,128)(2,1)} fusion(bf16[4,128,768]{2,1,0:T(8,128)(2,1)S(1)} %get-tuple-element.13, bf16[4,128,1536]{2,1,0:T(8,128)(2,1)S(1)} %bitcast.40), kind=kOutput, calls=%fused_computation | convolution fusion | flops 1212678144 | bytes 11796480 | tf_op jit(solution)/shard_map/tbf,tbd->tfd/dot_general | solution.py:496
  150.3 0.0 copy-done.2
  150.3 0.8 copy.65
  151.1 0.0 all-to-all-done.1
  151.1 1.0 convert_bitcast_fusion
  152.1 0.0 copy-start.9
  152.1 0.2 copy.63
  152.3 0.2 reshape.55
  152.6 0.2 copy-done.9
  152.8 30.0 %gather.1 = bf16[4,2,4,16,1664]{4,3,2,1,0:T(8,128)(2,1)S(1)} custom-call(bf16[4,16,1664]{2,1,0:T(8,128)(2,1)S(1)} %pad_maximum_fusion.own_ref), custom_call_target="tpu_custom_call" | custom-call | tf_op jit(solution)/shard_map/gather/pallas_call | solution.py:421
  182.8 2.3 %fusion = f32[4,128,1536]{2,1,0:T(8,128)} fusion(bf16[4,128,1664]{2,1,0:T(8,128)(2,1)S(1)} %bitcast.35), kind=kOutput, calls=%fused_computation.5 | convolution fusion | flops 201326592 | bytes 4849664 | tf_op jit(solution)/shard_map/tbc,tbd->tcd/dot_general | solution.py:507
  (9 shorter events, 0.2 us)
Async XLA Ops:
  0.6 20.1 %copy-start = (bf16[4,128,1536]{2,1,0:T(8,128)(2,1)S(1)}, bf16[4,128,1536]{2,1,0:T(8,128)(2,1)}, u32[]{:S(2)}) copy-start(bf16[4,128,1536]{2,1,0:T(8,128)(2,1)} %param.16) | copy-start | bytes 4718596
  0.6 4.7 %copy-start.14 = (s32[48]{0:T(128)S(1)}, s32[48]{0:T(128)}, u32[]{:S(2)}) copy-start(s32[48]{0:T(128)} %param.15) | copy-start | bytes 580
  20.2 0.6 copy-start.8
  20.8 4.8 %copy-start.10 = (f32[4,1536]{1,0:T(4,128)S(1)}, f32[4,1536]{1,0:T(4,128)}, u32[]{:S(2)}) copy-start(f32[4,1536]{1,0:T(4,128)} %param.17) | copy-start | bytes 73732
  20.8 5.4 %copy-start.13 = (f32[4,768]{1,0:T(4,128)S(1)}, f32[4,768]{1,0:T(4,128)}, u32[]{:S(2)}) copy-start(f32[4,768]{1,0:T(4,128)} %param.19) | copy-start | bytes 36868
  20.8 5.4 %copy-start.11 = (f32[4,1536]{1,0:T(4,128)S(1)}, f32[4,1536]{1,0:T(4,128)}, u32[]{:S(2)}) copy-start(f32[4,1536]{1,0:T(4,128)} %param.21) | copy-start | bytes 73732
  20.8 6.1 %copy-start.12 = (f32[4,1536]{1,0:T(4,128)S(1)}, f32[4,1536]{1,0:T(4,128)}, u32[]{:S(2)}) copy-start(f32[4,1536]{1,0:T(4,128)} %param.22) | copy-start | bytes 73732
  20.8 6.7 %copy-start.7 = (bf16[16,4,1536]{2,1,0:T(4,128)(2,1)S(1)}, bf16[16,4,1536]{2,1,0:T(4,128)(2,1)}, u32[]{:S(2)}) copy-start(bf16[16,4,1536]{2,1,0:T(4,128)(2,1)} %param.23) | copy-start | bytes 589828
  22.1 9.4 %all-to-all-start = ((bf16[4,16,16,96]{3,1,0,2:T(8,128)(2,1)}), bf16[4,16,16,96]{3,1,0,2:T(8,128)(2,1)S(1)}, u32[]{:S(2)}, u32[]{:S(2)}) async-start(bf16[4,16,16,96]{3,1,0,2:T(8,128)(2,1)} %copy.57), calls=%async_computation | async-start | bytes 524288 | tf_op jit(solution)/shard_map/all_to_all | solution.py:478
  32.5 0.7 copy-start.3
  33.3 0.7 copy-start.4
  34.0 0.7 copy-start.5
  129.8 0.7 copy-start.1
  133.1 18.0 %all-to-all-start.1 = ((bf16[4,16,16,96]{3,1,0,2:T(8,128)(2,1)}), bf16[4,16,16,96]{3,1,0,2:T(8,128)(2,1)}, u32[]{:S(2)}, u32[]{:S(2)}) async-start(bf16[4,16,16,96]{3,1,0,2:T(8,128)(2,1)} %copy.62), calls=%async_computation.1 | async-start | bytes 524288 | tf_op jit(solution)/shard_map/all_to_all | solution.py:478
  137.2 7.9 %copy-start.6 = (bf16[4,2,4,16,1536]{4,3,2,1,0:T(8,128)(2,1)S(1)}, bf16[4,2,4,16,1536]{4,3,2,1,0:T(8,128)(2,1)}, u32[]{:S(2)}) copy-start(bf16[4,2,4,16,1536]{4,3,2,1,0:T(8,128)(2,1)} %get-tuple-element.14) | copy-start | bytes 4718596
  145.1 5.2 %copy-start.2 = (bf16[4,16,1536]{2,1,0:T(8,128)(2,1)S(1)}, bf16[4,16,1536]{2,1,0:T(8,128)(2,1)}, u32[]{:S(2)}) copy-start(bf16[4,16,1536]{2,1,0:T(8,128)(2,1)} %copy-done.1) | copy-start | bytes 589828
  152.1 0.7 copy-start.9

commit v2 on v1

--- a/solution.py
+++ b/solution.py
@@ -37,13 +37,13 @@
     return jnp.sum(picked * keeper[:, :, None], axis=1)
 
 
-def remote(source, target, send, recv, peer):
+def remote(source, target, send, recv, peer, axis="batch"):
     return pltpu.make_async_remote_copy(
         src_ref=source,
         dst_ref=target,
         send_sem=send,
         recv_sem=recv,
-        device_id={"batch": peer},
+        device_id={axis: peer},
         device_id_type=pl.DeviceIdType.MESH,
     )
 
@@ -72,11 +72,10 @@
 
 
 class Gather:
-    def __init__(self, ring, own, full, local_sem, far_send, far_recv, near_send, near_recv):
+    def __init__(self, ring, own, full, one, many):
         self.ring, self.own, self.full = ring, own, full
-        self.local_sem = local_sem
-        self.far_send, self.far_recv = far_send, far_recv
-        self.near_send, self.near_recv = near_send, near_recv
+        self.local_sem, self.pass_send, self.pass_recv = one
+        self.far_send, self.far_recv, self.near_send, self.near_recv = many
 
     def far_copy(self, t, k):
         ring = self.ring
@@ -88,24 +87,37 @@
             ring.peer(k),
         )
 
+    def pass_copy(self, t, near):
+        ring = self.ring
+        return remote(
+            self.own.at[t],
+            self.full.at[t, near, ring.far],
+            self.pass_send.at[t],
+            self.pass_recv.at[t],
+            ring.partner,
+        )
+
     def own_copy(self, t):
         ring = self.ring
         return pltpu.make_async_copy(
             self.own.at[t], self.full.at[t, ring.near, ring.far], self.local_sem.at[t]
         )
 
-    def near_copy(self, t):
-        half = self.full.at[t, self.ring.near]
-        return remote(half, half, self.near_send.at[t], self.near_recv.at[t], self.ring.partner)
+    def near_copy(self, t, k, near):
+        ring = self.ring
+        block = self.full.at[t, near, ring.after(ring.far_count - k)]
+        return remote(
+            block, block, self.near_send.at[t, k - 1], self.near_recv.at[t, k - 1], ring.partner
+        )
 
     def start(self, t):
         for k in range(1, self.ring.far_count):
             self.far_copy(t, k).start()
+        self.pass_copy(t, self.ring.near).start()
         self.own_copy(t).start()
 
     def forward(self, t):
         ring = self.ring
-        self.own_copy(t).wait()
         for k in range(1, ring.far_count):
             remote(
                 self.own.at[t],
@@ -114,18 +126,19 @@
                 self.far_recv.at[t, k - 1],
                 ring.peer(k),
             ).wait_recv()
-        self.near_copy(t).start()
+            self.near_copy(t, k, ring.near).start()
 
     def arrive(self, t):
-        half = self.full.at[t, 1 - self.ring.near]
-        remote(
-            half, half, self.near_send.at[t], self.near_recv.at[t], self.ring.partner
-        ).wait_recv()
+        self.own_copy(t).wait()
+        self.pass_copy(t, 1 - self.ring.near).wait_recv()
+        for k in range(1, self.ring.far_count):
+            self.near_copy(t, k, 1 - self.ring.near).wait_recv()
 
     def finish(self, t):
+        self.pass_copy(t, self.ring.near).wait_send()
         for k in range(1, self.ring.far_count):
             self.far_copy(t, k).wait_send()
-        self.near_copy(t).wait_send()
+            self.near_copy(t, k, self.ring.near).wait_send()
 
 
 class Scatter:
@@ -228,13 +241,9 @@
         in_copy(t).start()
         out_copy(t).start()
     one = [one_sem.at[i] for i in range(10)]
-    many = [many_sem.at[i] for i in range(8)]
-    gather_a = Gather(
-        ring, normed_ref, normed_all_ref, one[0], many[0], many[1], one[1], one[2]
-    )
-    gather_b = Gather(
-        ring, upper_own, upper_all_ref, one[3], many[2], many[3], one[4], one[5]
-    )
+    many = [many_sem.at[i] for i in range(12)]
+    gather_a = Gather(ring, normed_ref, normed_all_ref, one[0:3], many[0:4])
+    gather_b = Gather(ring, upper_own, upper_all_ref, one[3:6], many[8:12])
     scatter_a = Scatter(
         ring, part_a, first_a, pair_a, second_a, one[6], one[7], many[4], many[5]
     )
@@ -260,7 +269,7 @@
                 normed_all_ref[t].reshape(examples, width),
                 in_held[t, :, columns],
                 preferred_element_type=jnp.float32,
-            ) + in_bias_ref[t, :, columns]
+            ) + in_bias_ref[pl.ds(t, 1), columns]
             factor = math.sqrt(2 / math.pi)
             square = value * value
             bent = jnp.tanh(factor * (value + 0.044715 * value * square))
@@ -282,12 +291,12 @@
         scatter_a.start(t)
 
     def turn(t):
-        output = scatter_a.total(t) + out_bias_ref[t] + normed_ref[t].astype(jnp.float32)
+        output = scatter_a.total(t) + out_bias_ref[pl.ds(t, 1), :] + normed_ref[t].astype(jnp.float32)
         center = output - jnp.mean(output, axis=-1, keepdims=True)
         scale_inv = lax.rsqrt(jnp.mean(center * center, axis=-1, keepdims=True) + epsilon)
-        result_ref[t] = (center * scale_inv * out_gain_ref[t]).astype(jnp.bfloat16)
+        result_ref[t] = (center * scale_inv * out_gain_ref[pl.ds(t, 1), :]).astype(jnp.bfloat16)
         upper_own[t] = normalize_back(
-            output, out_gain_ref[t], upstream_ref[t].astype(jnp.float32)
+            output, out_gain_ref[pl.ds(t, 1), :], upstream_ref[t].astype(jnp.float32)
         ).astype(jnp.bfloat16)
         gather_b.start(t)
 
@@ -322,7 +331,7 @@
 
     def close(t):
         normed_grad = scatter_b.total(t) + upper_own[t].astype(jnp.float32)
-        sum_grad_ref[t] = normalize_back(summed_ref[t], mix_gain_ref[t], normed_grad).astype(
+        sum_grad_ref[t] = normalize_back(summed_ref[t], mix_gain_ref[pl.ds(t, 1), :], normed_grad).astype(
             jnp.bfloat16
         )
 
@@ -388,7 +397,7 @@
             *one_way,
             pltpu.SemaphoreType.DMA((2, tokens)),
             pltpu.SemaphoreType.DMA((10, tokens)),
-            pltpu.SemaphoreType.DMA((8, tokens, far_count - 1)),
+            pltpu.SemaphoreType.DMA((12, tokens, far_count - 1)),
         ],
         compiler_params=pltpu.CompilerParams(
             collective_id=0, has_side_effects=True, vmem_limit_bytes=50 * 1024 * 1024
@@ -400,8 +409,11 @@
 def gather_kernel(count, own_ref, full_ref, one_sem, many_sem):
     ring = Ring(count)
     gather = Gather(
-        ring, own_ref, full_ref, one_sem.at[0], many_sem.at[0], many_sem.at[1], one_sem.at[1],
-        one_sem.at[2],
+        ring,
+        own_ref,
+        full_ref,
+        [one_sem.at[i] for i in range(3)],
+        [many_sem.at[i] for i in range(4)],
     )
     ring.greet()
     tokens = own_ref.shape[0]
@@ -425,13 +437,105 @@
         out_specs=vmem,
         scratch_shapes=[
             pltpu.SemaphoreType.DMA((3, tokens)),
-            pltpu.SemaphoreType.DMA((2, tokens, far_count - 1)),
+            pltpu.SemaphoreType.DMA((4, tokens, far_count - 1)),
         ],
         compiler_params=pltpu.CompilerParams(
             collective_id=1, has_side_effects=True, vmem_limit_bytes=16 * 1024 * 1024
         ),
         name="gather",
     )(own)
+
+
+def mix_kernel(
+    peers,
+    part_ref,
+    projection_ref,
+    grouped_ref,
+    own_ref,
+    moved_ref,
+    arrived,
+    blocks,
+    sems,
+):
+    rank = lax.axis_index("tok")
+    tokens, _, width = projection_ref.shape
+    piece = width // peers
+    after = lambda step: (rank + step) % peers
+    barrier = pltpu.get_barrier_semaphore()
+    for k in range(1, peers):
+        pl.semaphore_signal(
+            barrier, inc=1, device_id={"tok": after(k)}, device_id_type=pl.DeviceIdType.MESH
+        )
+    pl.semaphore_wait(barrier, peers - 1)
+
+    def part_copy(k):
+        return remote(
+            part_ref.at[after(k)],
+            arrived.at[k - 1],
+            sems.at[0, k - 1],
+            sems.at[1, k - 1],
+            after(k),
+            "tok",
+        )
+
+    def slice_copy(k, slot):
+        return remote(
+            blocks.at[after(k)],
+            moved_ref.at[slot],
+            sems.at[2, k - 1],
+            sems.at[3, k - 1],
+            after(k),
+            "tok",
+        )
+
+    for k in range(1, peers):
+        part_copy(k).start()
+    total = part_ref[rank]
+    for k in range(1, peers):
+        part_copy(k).wait_recv()
+        total = total + arrived[k - 1]
+    grouped_ref[...] = total.astype(jnp.bfloat16)
+    for t in range(tokens):
+        value = jnp.dot(
+            grouped_ref[t], projection_ref[t], preferred_element_type=jnp.float32
+        ).astype(jnp.bfloat16)
+        own_ref[t] = value
+        for peer in range(peers):
+            blocks[peer, t] = value[:, peer * piece : (peer + 1) * piece]
+    for k in range(1, peers):
+        slice_copy(k, rank).start()
+    moved_ref[rank] = blocks[rank]
+    for k in range(1, peers):
+        slice_copy(k, after(peers - k)).wait_recv()
+    for k in range(1, peers):
+        part_copy(k).wait_send()
+        slice_copy(k, rank).wait_send()
+
+
+def run_mix(peers, part, projection):
+    tokens, embed, width = projection.shape
+    rows = part.shape[1]
+    vmem = pl.BlockSpec(memory_space=pltpu.VMEM)
+    moved = (peers, tokens, rows, width // peers)
+    return pl.pallas_call(
+        functools.partial(mix_kernel, peers),
+        out_shape=[
+            jax.ShapeDtypeStruct((tokens, rows, embed), jnp.bfloat16),
+            jax.ShapeDtypeStruct((tokens, rows, width), jnp.bfloat16),
+            jax.ShapeDtypeStruct(moved, jnp.bfloat16),
+        ],
+        in_specs=[vmem] * 2,
+        out_specs=[vmem] * 3,
+        scratch_shapes=[
+            pltpu.VMEM((peers - 1, tokens, rows, embed), jnp.float32),
+            pltpu.VMEM(moved, jnp.bfloat16),
+            pltpu.SemaphoreType.DMA((4, peers - 1)),
+        ],
+        compiler_params=pltpu.CompilerParams(
+            collective_id=2, has_side_effects=True, vmem_limit_bytes=16 * 1024 * 1024
+        ),
+        name="mix",
+    )(part.reshape(peers, tokens, rows, embed), projection)
 
 
 def local(
@@ -467,29 +571,29 @@
         jnp.float32
     )
     partial_groups = jnp.einsum("fbc,ft->tbc", pooled, selector, precision=lax.Precision.HIGHEST)
-    group_all = lax.psum(partial_groups, "tok").astype(jnp.bfloat16)
-    grouped = lax.dynamic_slice_in_dim(group_all, token_rank * local_tokens, local_tokens, 0)
-    own_tokens = jnp.einsum(
-        "tbc,tcd->tbd", grouped, projection, preferred_element_type=jnp.float32
-    ).astype(jnp.bfloat16)
+    grouped, own_tokens, moved_tokens = run_mix(lax.axis_size("tok"), partial_groups, projection)
+
+    def unfold(moved):
+        blocks = moved.reshape(all_tokens, local_rows, local_tokens, head_dim)
+        return jnp.transpose(blocks, (2, 1, 0, 3)).reshape(local_tokens, local_rows, model_width)
 
     def exchange(values):
         blocks = values.reshape(local_tokens, local_rows, all_tokens, head_dim)
         moved = lax.all_to_all(blocks, "tok", split_axis=2, concat_axis=0, tiled=True)
-        return jnp.transpose(moved, (2, 1, 0, 3)).reshape(values.shape)
-
-    summed = exchange(own_tokens).astype(jnp.float32) + own_tokens.astype(jnp.float32)
+        return unfold(moved)
+
+    summed = unfold(moved_tokens).astype(jnp.float32) + own_tokens.astype(jnp.float32)
     normed = normalize(summed, mix_gain[:, None]).astype(jnp.bfloat16)
     result, normed_all, hidden, upper_all, hidden_grad, sum_grad = run_block(
         count,
         normed,
         summed,
-        mix_gain[:, None],
+        mix_gain,
         in_weight,
-        in_bias[:, None],
+        in_bias,
         out_weight,
-        out_bias[:, None],
-        out_gain[:, None],
+        out_bias,
+        out_gain,
         jnp.transpose(upstream, (1, 0, 2)),
     )
     flat = (local_tokens, count * local_rows, model_width)

time: 186 us -> 164 us (0.88)
  blocking collectives: 14.5 us -> 0 us
  Pallas kernels: 125 us -> 130 us
  waiting for transfers between devices: 4.02 us -> 0.01 us
  starting transfers between devices: 7.44 us -> 4.05 us
  local copies, waits for them, and re-layouts: 12.2 us -> 8.94 us
    psum x1 -> x0, blocking collectives: 14.5 us -> none  [local(): group_all = lax.psum(partial_groups, 'tok').astype(jnp.bfloat16)]
    pallas_call x0 -> x1, Pallas kernels: none -> 10.1 us  [run_mix(): pl.pallas_call(functools.partial(mix_kernel, peers), out_shape=[jax.Shape...]
    all_to_all x2 -> x1, waiting for transfers between devices: 4.02 us -> 0.01 us  [exchange(): lax.all_to_all(blocks, 'tok', split_axis=2, concat_axis=0, tiled=True)]
    pallas_call x1, Pallas kernels: 30 us -> 26.2 us  [run_gather(): pl.pallas_call(functools.partial(gather_kernel, count), out_shape=jax.Sha...]
    all_to_all x2 -> x1, starting transfers between devices: 7.44 us -> 4.05 us  [exchange(): lax.all_to_all(blocks, 'tok', split_axis=2, concat_axis=0, tiled=True)]
    broadcast_in_dim x4 -> x0, local copies, waits for them, and re-layouts: 1.89 us -> none  [the longest x1 0.63 us: local(): normed = normalize(summed, mix_gain[:, None]).astype(jnp.bfloat16)]
    unnamed x33 -> x23, local copies, waits for them, and re-layouts: 5.5 us -> 4.75 us
  transfers between devices with their start and end apart: 2 -> 1, of which waited for: 1 -> 0; matrix products, arithmetic and copies ran while one was open for 9% -> 9% of each run, Pallas kernels for 0% -> 0%
where the time goes in v2:
time: 164 us; the launch traced here: 163 us
  Pallas kernels  130 us (79%)
  matrix products  15.9 us (10%)
  local copies, waits for them, and re-layouts  8.94 us (5%)
  starting transfers between devices  4.05 us (2%)
  other arithmetic  3.35 us (2%)
    pallas_call x1, Pallas kernels, run_block(): pl.pallas_call(functools.partial(block_kernel, count), out_shape=[jax.Sha...  94 us
    pallas_call x1, Pallas kernels, run_gather(): pl.pallas_call(functools.partial(gather_kernel, count), out_shape=jax.Sha...  26.2 us
    pallas_call x1, Pallas kernels, run_mix(): pl.pallas_call(functools.partial(mix_kernel, peers), out_shape=[jax.Shape...  10.1 us
    dot_general x1, matrix products, local(): jnp.einsum('tbd,tbf->tdf', normed_all.reshape(flat), hidden_grad, preferr...  7.91 us
    dot_general x1, matrix products, local(): jnp.einsum('tbf,tbd->tfd', hidden, upper_all.reshape(flat), preferred_ele...  5.17 us
    unnamed x23, local copies, waits for them, and re-layouts  4.75 us
    all_to_all x1, starting transfers between devices, exchange(): lax.all_to_all(blocks, 'tok', split_axis=2, concat_axis=0, tiled=True)  4.05 us
  transfers between devices with their start and end apart: 1, of which 0 were waited for; matrix products, arithmetic and copies ran while one was open for 9% of the time, Pallas kernels for 0%

profile of v2, /device:TPU:0, one launch (start us, length us, event | category | flops | bytes accessed | tf_op | source)
XLA Modules:
  0.0 163.4 jit_solution(3004301389534368500)
XLA Ops:
  0.6 0.0 copy-start
  0.6 0.0 copy-start.9
  0.7 0.0 copy-start.1
  0.7 0.9 copy.50
  1.6 0.8 fusion.6
  2.4 0.1 copy.51
  2.5 1.0 convert_reduce_fusion
  3.6 0.0 copy-done
  3.6 0.4 fusion.2
  4.0 0.0 copy-done.9
  4.0 0.1 dynamic_slice.3
  4.1 0.2 fusion.4
  4.3 0.0 copy-done.1
  4.3 10.1 %mix.1 = (bf16[4,16,128]{2,1,0:T(8,128)(2,1)S(1)}, bf16[4,16,1536]{2,1,0:T(8,128)(2,1)S(1)}, bf16[4,4,16,384]{3,2,1,0:T(8,128)(2,1)S(1)}) custom-call(f32[4,4,16,128]{3,2,1,0:T(8,128)S(1)} %bitcast.34, bf16[4,128,1536]{2,1,0:T(8,128)(2,1)S(1)} %copy-done.1), custom_call_target="tpu_custom_call" | custom-call | tf_op jit(solution)/shard_map/mix/pallas_call | solution.py:520
  14.4 0.3 reshape.57
  14.7 0.0 copy-start.8
  14.8 0.0 copy-start.2
  14.8 0.3 copy.72
  15.1 0.2 reshape.55
  15.3 0.1 fusion.10
  15.5 0.2 multiply_reduce_fusion
  15.7 0.0 copy-done.8
  15.7 0.0 copy-done.2
  15.7 0.1 multiply_convert_fusion.normed_ref
  15.9 0.0 copy-start.3
  15.9 0.7 copy-done.3
  16.6 0.0 copy-start.4
  16.6 0.7 copy-done.4
  17.3 0.0 copy-start.5
  17.3 0.7 copy-done.5
  18.1 0.0 copy-start.6
  18.1 0.7 copy-done.6
  18.8 94.0 %block.1 = (bf16[4,16,1536]{2,1,0:T(8,128)(2,1)S(1)}, bf16[4,2,4,16,1536]{4,3,2,1,0:T(8,128)(2,1)}, bf16[4,128,768]{2,1,0:T(8,128)(2,1)S(1)}, bf16[4,2,4,16,1536...) custom-call(bf16[4,16,1536]{2,1,0:T(8,128)(2,1)S(1)} %multiply_convert_fusion.normed_ref, ...), custom_call_target="tpu_custom_call" | custom-call | tf_op jit(solution)/shard_map/block/pallas_call | solution.py:379
  112.8 0.9 reshape.53
  113.7 1.7 %copy.59 = bf16[4,16,16,96]{3,1,0,2:T(8,128)(2,1)} copy(bf16[4,16,16,96]{3,2,1,0:T(8,128)(2,1)} %reshape.53) | data formatting | bytes 393216 | tf_op jit(solution)/shard_map/reshape | solution.py:581
  115.4 4.0 %all-to-all-start = ((bf16[4,16,16,96]{3,1,0,2:T(8,128)(2,1)}), bf16[4,16,16,96]{3,1,0,2:T(8,128)(2,1)}, u32[]{:S(2)}, u32[]{:S(2)}) async-start(bf16[4,16,16,96]{3,1,0,2:T(8,128)(2,1)} %copy.59), calls=%async_computation | async-start | bytes 524288 | tf_op jit(solution)/shard_map/all_to_all | solution.py:582
  119.5 0.0 copy-start.7
  119.5 7.9 %convolution_convert_fusion.1 = bf16[4,1536,768]{2,1,0:T(8,128)(2,1)} fusion(bf16[4,128,1536]{2,1,0:T(8,128)(2,1)} %bitcast.39, bf16[4,128,768]{2,1,0:T(8,128)(2,1)S(1)} %get-tuple-element.17), kind=kOutput, calls=%fused_computation.1 | convolution fusion | flops 1212678144 | bytes 11796480 | tf_op jit(solution)/shard_map/tbd,tbf->tdf/dot_general | solution.py:603
  127.4 0.0 copy-done.7
  127.4 5.2 %convolution_convert_fusion = bf16[4,768,1536]{2,1,0:T(8,128)(2,1)} fusion(bf16[4,128,768]{2,1,0:T(8,128)(2,1)S(1)} %get-tuple-element.18, bf16[4,128,1536]{2,1,0:T(8,128)(2,1)S(1)} %bitcast.38), kind=kOutput, calls=%fused_computation | convolution fusion | flops 1212678144 | bytes 11796480 | tf_op jit(solution)/shard_map/tbf,tbd->tfd/dot_general | solution.py:600
  132.6 0.8 copy.62
  133.4 0.0 all-to-all-done
  133.4 1.0 convert_bitcast_fusion
  134.4 0.2 copy.60
  134.6 0.2 reshape.56
  134.9 26.2 %gather.1 = bf16[4,2,4,16,1664]{4,3,2,1,0:T(8,128)(2,1)S(1)} custom-call(bf16[4,16,1664]{2,1,0:T(8,128)(2,1)S(1)} %pad_maximum_fusion.own_ref), custom_call_target="tpu_custom_call" | custom-call | tf_op jit(solution)/shard_map/gather/pallas_call | solution.py:433
  161.2 2.3 %fusion = f32[4,128,1536]{2,1,0:T(8,128)} fusion(bf16[4,128,1664]{2,1,0:T(8,128)(2,1)S(1)} %bitcast.32), kind=kOutput, calls=%fused_computation.4 | convolution fusion | flops 201326592 | bytes 4849664 | tf_op jit(solution)/shard_map/tbc,tbd->tcd/dot_general | solution.py:611
  (6 shorter events, 0.2 us)
Async XLA Ops:
  0.6 2.9 %copy-start = (bf16[12,512,128]{2,1,0:T(8,128)(2,1)S(1)}, bf16[12,512,128]{2,1,0:T(8,128)(2,1)}, u32[]{:S(2)}) copy-start(bf16[12,512,128]{2,1,0:T(8,128)(2,1)} %param.12) | copy-start | bytes 4718596
  0.6 3.3 %copy-start.9 = (s32[48]{0:T(128)S(1)}, s32[48]{0:T(128)}, u32[]{:S(2)}) copy-start(s32[48]{0:T(128)} %param.15) | copy-start | bytes 580
  0.7 3.7 %copy-start.1 = (bf16[4,128,1536]{2,1,0:T(8,128)(2,1)S(1)}, bf16[4,128,1536]{2,1,0:T(8,128)(2,1)}, u32[]{:S(2)}) copy-start(bf16[4,128,1536]{2,1,0:T(8,128)(2,1)} %projection_ref.1) | copy-start | bytes 4718596
  14.7 0.9 copy-start.8
  14.8 1.0 copy-start.2
  15.9 0.7 copy-start.3
  16.6 0.7 copy-start.4
  17.3 0.7 copy-start.5
  18.1 0.7 copy-start.6
  115.4 18.0 %all-to-all-start = ((bf16[4,16,16,96]{3,1,0,2:T(8,128)(2,1)}), bf16[4,16,16,96]{3,1,0,2:T(8,128)(2,1)}, u32[]{:S(2)}, u32[]{:S(2)}) async-start(bf16[4,16,16,96]{3,1,0,2:T(8,128)(2,1)} %copy.59), calls=%async_computation | async-start | bytes 524288 | tf_op jit(solution)/shard_map/all_to_all | solution.py:582
  119.5 7.9 %copy-start.7 = (bf16[4,2,4,16,1536]{4,3,2,1,0:T(8,128)(2,1)S(1)}, bf16[4,2,4,16,1536]{4,3,2,1,0:T(8,128)(2,1)}, u32[]{:S(2)}) copy-start(bf16[4,2,4,16,1536]{4,3,2,1,0:T(8,128)(2,1)} %get-tuple-element.19) | copy-start | bytes 4718596
